TPU v7x, 32 devices: a whole 2x2x4 slice. The times are simulated.
32 devices in a mesh: gx: 4 (over y, x), gy: 8 (over z, core).
Axes of the slice: x: 2, y: 2, z: 4, core: 2. Of those that a mesh axis runs over, the one named last changes fastest.
Arguments:
- schur_blocks: float32 [32, 2048, 2048], P(('gx', 'gy')), may hold values from -1 to 11, as said below
- offsets: int32 [32], P(('gx', 'gy')), may hold values from 256 to 768, as said below
- right_side: float32 [32768, 128], P(('gx', 'gy')), may hold values from -20 to 20
- coarse_basis: float32 [32768, 128], P(('gx', 'gy')), may hold values from -0.03125 to 0.03125
- coarse_load: float32 [128, 128], replicated, may hold values from -6 to 6
Outputs:
- multipliers: float32 [32768, 128], P(('gx', 'gy'))
- amplitudes: float32 [128, 128], replicated
Inputs may be any that keep to these rules, and one draw needn't show every extreme that they name: `schur_blocks`: each block is symmetric positive definite. `offsets`: both ends of the range are taken by some subdomain.
All inputs are finite; a program needn't handle non-finite values.
Results may differ from a plain program's by a relative error of at most 0.0003.
Values sent between devices are 32-bit elements; how exact they have to be, the bound alone decides.
A program may use at most 128 MiB of HBM per device.

v0:
```python
import functools

import jax
import jax.numpy as jnp
from jax import lax
from jax.experimental import pallas as pl
from jax.experimental.pallas import tpu as pltpu
from jax.sharding import PartitionSpec as P

ITERS = 3
MESH = pl.DeviceIdType.MESH
HIGHEST = lax.Precision.HIGHEST
F32 = jnp.float32
BF16 = jnp.bfloat16
CHUNK = 128
SLOTS = 4
BLOCK = 512
EXCHANGES = 2 * ITERS + 2
REDUCES = 2 + ITERS


def dot(a, b):
    return jnp.dot(a, b, precision=HIGHEST, preferred_element_type=F32)


def kernel(
    nx, ny, off_ref, schur_ref, right_ref, basis_ref, load_ref, lam_ref, amp_ref,
    stage, s_hi, s_lo, vec, twice, basis_w, basis_t, fc_own, fc_w, fc_t, right_w, z, d, p_old, image_old, own,
    out_l, out_r, in_l, in_r, part, fold, total, m_ref, sweep, scal_in, scal_all,
    stage_sem, hs_l, hs_r, hr_l, hr_r, fold_s, fold_r, tot_s, tot_r, scal_s, scal_r,
):
    n = nx * ny
    slab = right_ref.shape[0]
    nc = basis_ref.shape[1]
    width = 2 * slab
    low = slab // 4
    span = slab - low
    me = lax.axis_index("gx") * ny + lax.axis_index("gy")
    off = off_ref[0]
    chunks = width // CHUNK

    def where_is(i):
        return (lax.div(i, ny), lax.rem(i, ny))

    def fetch(i, slot):
        return pltpu.make_async_copy(
            schur_ref.at[pl.ds(i * CHUNK, CHUNK), :], stage.at[slot], stage_sem.at[slot]
        )

    for i in range(SLOTS):
        fetch(i, i).start()

    @pl.when(me == 0)
    def _():
        in_l[...] = jnp.zeros_like(in_l)

    @pl.when(me == n - 1)
    def _():
        in_r[...] = jnp.zeros_like(in_r)

    barrier = pltpu.get_barrier_semaphore()

    def greet(k, carry):
        pl.semaphore_signal(barrier, inc=1, device_id=where_is(lax.rem(me + k, n)), device_id_type=MESH)
        return carry

    lax.fori_loop(1, n, greet, 0)
    pl.semaphore_wait(barrier, n - 1)

    def to_right(e, src):
        return pltpu.make_async_remote_copy(
            src_ref=src, dst_ref=in_l.at[e], send_sem=hs_r.at[e], recv_sem=hr_l.at[e],
            device_id=where_is(lax.rem(me + 1, n)), device_id_type=MESH,
        )

    def to_left(e, src):
        return pltpu.make_async_remote_copy(
            src_ref=src, dst_ref=in_r.at[e], send_sem=hs_l.at[e], recv_sem=hr_r.at[e],
            device_id=where_is(lax.rem(me + n - 1, n)), device_id_type=MESH,
        )

    def send_halo(e, src_l, src_r):
        @pl.when(me > 0)
        def _():
            to_left(e, src_l).start()

        @pl.when(me < n - 1)
        def _():
            to_right(e, src_r).start()

    def wait_halo(e):
        @pl.when(me > 0)
        def _():
            to_right(e, out_r.at[0]).wait_recv()

        @pl.when(me < n - 1)
        def _():
            to_left(e, out_l.at[0]).wait_recv()

    def wait_sent(e):
        @pl.when(me > 0)
        def _():
            to_left(e, out_l.at[0]).wait_send()

        @pl.when(me < n - 1)
        def _():
            to_right(e, out_r.at[0]).wait_send()

    def rows_below(first, count):
        return lax.broadcasted_iota(jnp.int32, (count, nc), 0) + first < off

    def folded_halo(e, first, count):
        mask = rows_below(first, count)
        right = in_r[e, pl.ds(first, count), :] if first + count <= span else jnp.zeros((count, nc), F32)
        left = in_l[e, pl.ds(first - low, count), :] if first >= low else jnp.zeros((count, nc), F32)
        return jnp.where(mask, right, left)

    def folded(e):
        return jnp.concatenate([folded_halo(e, i * low, low) for i in range(slab // low)], axis=0)

    def apply_block(src):
        twice[0:width, :] = src[...]
        twice[width:, :] = src[...]
        window = twice[pl.ds(off, width), :]
        hi = window.astype(BF16)
        vec[:, :nc] = hi
        vec[:, nc:] = (window - hi.astype(F32)).astype(BF16)

        def rows(i, carry):
            at = pl.ds(pl.multiple_of(i * BLOCK, BLOCK), BLOCK)
            both = jnp.dot(s_hi[at, :], vec[...], preferred_element_type=F32)
            rest = jnp.dot(s_lo[at, :], vec[:, :nc], preferred_element_type=F32)
            result = both[:, :nc] + (both[:, nc:] + rest)
            twice[at, :] = result
            twice[pl.ds(pl.multiple_of(width + i * BLOCK, BLOCK), BLOCK), :] = result
            return carry

        lax.fori_loop(0, width // BLOCK, rows, 0)

    def folded_product():
        return twice[pl.ds(width - off, width), :]

    def send_parts(e, k, product):
        mask = rows_below(0, slab)
        head = product[:slab]
        out_l[k] = jnp.where(mask, 0.0, head)[low:]
        out_r[k] = jnp.where(mask, head, 0.0)[:span]
        send_halo(e, out_l.at[k], out_r.at[k])

    def assemble(e, product):
        wait_halo(e)
        left = in_l[e]
        right = in_r[e]
        mine = product[slab:]
        return jnp.concatenate(
            [
                mine[:low] + left[:low],
                mine[low:span] + (left[low:] + right[: span - low]),
                mine[span:] + right[span - low :],
            ],
            axis=0,
        )

    def reduce_start(r, value):
        rows = value.shape[0]
        p = rows // n
        for i in range(n):
            part[r][i] = value[i * p : (i + 1) * p]

        def send(k, carry):
            peer = lax.rem(me + k, n)
            pltpu.make_async_remote_copy(
                src_ref=part[r].at[peer], dst_ref=fold[r].at[me], send_sem=fold_s.at[r],
                recv_sem=fold_r.at[r], device_id=where_is(peer), device_id_type=MESH,
            ).start()
            return carry

        lax.fori_loop(1, n, send, 0)
        fold[r][me] = part[r][me]

    def reduce_turn(r):
        arrived = fold[r].at[pl.ds(0, n - 1)]
        pltpu.make_async_copy(arrived, arrived, fold_r.at[r]).wait()
        total[r][me] = jnp.sum(fold[r][...], axis=0)

        def send(k, carry):
            peer = lax.rem(me + k, n)
            pltpu.make_async_remote_copy(
                src_ref=total[r].at[me], dst_ref=total[r].at[me], send_sem=tot_s.at[r],
                recv_sem=tot_r.at[r], device_id=where_is(peer), device_id_type=MESH,
            ).start()
            return carry

        lax.fori_loop(1, n, send, 0)

    def reduce_end(r):
        arrived = total[r].at[pl.ds(0, n - 1)]
        pltpu.make_async_copy(arrived, arrived, tot_r.at[r]).wait()
        p = total[r].shape[1]
        for i in range(n):
            m_ref[i * p : (i + 1) * p, :] = total[r][i]
        return m_ref[: n * p, :]

    def scal_start(it):
        scal_all[it, me] = scal_in[it]

        def send(k, carry):
            peer = lax.rem(me + k, n)
            pltpu.make_async_remote_copy(
                src_ref=scal_in.at[it], dst_ref=scal_all.at[it, me], send_sem=scal_s.at[it],
                recv_sem=scal_r.at[it], device_id=where_is(peer), device_id_type=MESH,
            ).start()
            return carry

        lax.fori_loop(1, n, send, 0)

    def scal_end(it):
        arrived = scal_all.at[it, pl.ds(0, n - 1)]
        pltpu.make_async_copy(arrived, arrived, scal_r.at[it]).wait()
        sums = jnp.sum(scal_all[it], axis=0)
        return sums[0:1], sums[1:2], sums[2:3]

    send_halo(0, basis_ref.at[pl.ds(0, span)], basis_ref.at[pl.ds(low, span)])
    basis_t[...] = basis_ref[...].T
    both = jnp.concatenate([basis_ref[...], right_ref[...]], axis=1)
    local = dot(basis_t[...], both)
    reduce_start(0, jnp.concatenate([local[:, :nc], local[:, nc:]], axis=0))

    def split(i, carry):
        slot = lax.rem(i, SLOTS)
        fetch(i, slot).wait()
        at = pl.ds(pl.multiple_of(i * CHUNK, CHUNK), CHUNK)
        value = stage[slot]
        hi = value.astype(BF16)
        s_hi[at, :] = hi
        s_lo[at, :] = (value - hi.astype(F32)).astype(BF16)

        @pl.when(i + SLOTS < chunks)
        def _():
            fetch(i + SLOTS, slot).start()

        return carry

    lax.fori_loop(0, chunks, split, 0)
    reduce_turn(0)

    wait_halo(0)
    basis_w[0:slab, :] = folded(0)
    basis_w[slab:, :] = basis_ref[...]
    apply_block(basis_w)
    product = folded_product()
    send_parts(2, 0, product)
    fc_own[...] = assemble(2, product)
    send_halo(3, fc_own.at[pl.ds(0, span)], fc_own.at[pl.ds(low, span)])
    reduce_start(1, dot(basis_t[...], fc_own[...]))
    fc_t[...] = fc_own[...].T
    gram = reduce_end(0)
    sweep[...] = gram[:nc]
    right_coarse = gram[nc:]
    reduce_turn(1)
    send_halo(1, right_ref.at[pl.ds(0, span)], right_ref.at[pl.ds(low, span)])

    lanes = lax.broadcasted_iota(jnp.int32, (nc, nc), 1)
    subs = lax.broadcasted_iota(jnp.int32, (nc, nc), 0)

    def eliminate(a, k, row, col, p):
        here = lanes == k
        inverse = 1.0 / p
        scaled = row * inverse
        new = a - col * scaled
        new = jnp.where(here, col * inverse, new)
        return jnp.where(subs == k, jnp.where(here, -inverse, scaled), new), scaled, inverse

    def pick(row, k):
        return jnp.sum(jnp.where(lanes[:1] == k, row, 0.0), axis=1, keepdims=True)

    def pivot(half, a):
        k = 2 * half
        row1, row2 = sweep[pl.ds(k, 1), :], sweep[pl.ds(k + 1, 1), :]
        col1 = jnp.sum(jnp.where(lanes == k, a, 0.0), axis=1, keepdims=True)
        col2 = jnp.sum(jnp.where(lanes == k + 1, a, 0.0), axis=1, keepdims=True)
        p1, cross, p2 = pick(row1, k), pick(row1, k + 1), pick(row2, k + 1)
        a, scaled, inverse = eliminate(a, k, row1, col1, p1)
        ratio = cross * inverse
        row2 = jnp.where(lanes[:1] == k, ratio, row2 - cross * scaled)
        col2 = jnp.where(subs[:, :1] == k, ratio, col2 - col1 * ratio)
        a, _, _ = eliminate(a, k + 1, row2, col2, p2 - cross * ratio)
        sweep[...] = a
        return a

    ginv = -lax.fori_loop(0, nc // 2, pivot, sweep[...])

    y0 = dot(ginv, load_ref[...])
    lam_ref[...] = dot(basis_ref[...], y0)
    cfc = reduce_end(1)
    amp = dot(ginv, right_coarse - dot(cfc, y0))
    wait_halo(1)
    wait_halo(3)
    right_w[0:slab, :] = folded(1)
    right_w[slab:, :] = right_ref[...]
    fc_w[0:slab, :] = folded(3)
    fc_w[slab:, :] = fc_own[...]
    z[...] = right_w[...] - dot(fc_w[...], y0) - dot(basis_w[...], amp)

    energy = curvature = coarse_image = None
    for it in range(ITERS):
        last = it == ITERS - 1
        reduce_start(2 + it, dot(fc_t[...], z[slab:, :]))
        apply_block(z)
        product = folded_product()
        e = 4 + 2 * it
        if not last:
            send_parts(e, 1 + it, product)
        scal_in[it, 0:1] = jnp.sum(z[...] * product, axis=0, keepdims=True)
        scal_in[it, 1:2] = jnp.sum(z[slab:, :] * z[slab:, :], axis=0, keepdims=True)
        if it == 0:
            scal_in[it, 2:3] = jnp.zeros((1, nc), F32)
        else:
            scal_in[it, 2:3] = jnp.sum(z[...] * p_old[...], axis=0, keepdims=True)
        scal_in[it, 3:4] = jnp.zeros((1, nc), F32)
        scal_start(it)
        reduce_turn(2 + it)
        if not last:
            own[it] = assemble(e, product)
            send_halo(e + 1, own.at[it, pl.ds(0, span)], own.at[it, pl.ds(low, span)])
        curved, energy_now, crossed = scal_end(it)
        coarse_now = reduce_end(2 + it)
        if it == 0:
            d[...] = z[slab:, :]
            curvature = curved
            coarse_image = coarse_now
            if not last:
                p_old[...] = product
        else:
            beta = energy_now / energy
            d[...] = z[slab:, :] + beta * d[...]
            curvature = curved + beta * (2.0 * crossed + beta * curvature)
            coarse_image = coarse_now + beta * coarse_image
            if not last:
                p_old[...] = product + beta * p_old[...]
        energy = energy_now
        step = energy / curvature
        lam_ref[...] += step * d[...]
        shift = dot(ginv, coarse_image)
        amp = amp - step * shift
        if not last:
            wait_halo(e + 1)
            whole = jnp.concatenate([folded(e + 1), own[it]], axis=0)
            if it > 0:
                whole = whole + beta * image_old[...]
            image_old[...] = whole
            z[...] = z[...] - step * (whole - dot(basis_w[...], shift))
    amp_ref[...] = amp

    for e in range(EXCHANGES):
        wait_sent(e)
    for r in range(REDUCES):
        sent = fold[r].at[pl.ds(0, n - 1)]
        pltpu.make_async_copy(sent, sent, fold_s.at[r]).wait()
        sent = total[r].at[pl.ds(0, n - 1)]
        pltpu.make_async_copy(sent, sent, tot_s.at[r]).wait()
    for it in range(ITERS):
        sent = scal_all.at[it, pl.ds(0, n - 1)]
        pltpu.make_async_copy(sent, sent, scal_s.at[it]).wait()


def entry(nx, ny, groups, *refs):
    fixed = refs[: groups[0]]
    rest = refs[groups[0] :]
    part, rest = rest[:REDUCES], rest[REDUCES:]
    fold, rest = rest[:REDUCES], rest[REDUCES:]
    total, rest = rest[:REDUCES], rest[REDUCES:]
    kernel(nx, ny, *fixed, part, fold, total, *rest)


def solution(mesh):
    nx, ny = mesh.shape["gx"], mesh.shape["gy"]
    n = nx * ny

    def local(schur_blocks, offsets, right_side, coarse_basis, coarse_load):
        slab, r = right_side.shape
        nc = coarse_basis.shape[1]
        width = schur_blocks.shape[1]
        span = slab - slab // 4
        row_counts = [2 * nc] + [nc] * (REDUCES - 1)

        def pieces():
            return [pltpu.VMEM((n, rows // n, r), F32) for rows in row_counts]

        vmem = pl.BlockSpec(memory_space=pltpu.VMEM)
        fixed = [
            pltpu.VMEM((SLOTS, CHUNK, width), F32),
            pltpu.VMEM((width, width), BF16),
            pltpu.VMEM((width, width), BF16),
            pltpu.VMEM((width, 2 * r), BF16),
            pltpu.VMEM((2 * width, r), F32),
            pltpu.VMEM((width, nc), F32),
            pltpu.VMEM((nc, slab), F32),
            pltpu.VMEM((slab, nc), F32),
            pltpu.VMEM((width, nc), F32),
            pltpu.VMEM((nc, slab), F32),
            pltpu.VMEM((width, r), F32),
            pltpu.VMEM((width, r), F32),
            pltpu.VMEM((slab, r), F32),
            pltpu.VMEM((width, r), F32),
            pltpu.VMEM((width, r), F32),
            pltpu.VMEM((ITERS - 1, slab, r), F32),
            pltpu.VMEM((ITERS, span, r), F32),
            pltpu.VMEM((ITERS, span, r), F32),
            pltpu.VMEM((EXCHANGES, span, r), F32),
            pltpu.VMEM((EXCHANGES, span, r), F32),
        ]
        dma = pltpu.SemaphoreType.DMA
        rest = [
            pltpu.VMEM((2 * nc, r), F32),
            pltpu.VMEM((nc, nc), F32),
            pltpu.VMEM((ITERS, 4, r), F32),
            pltpu.VMEM((ITERS, n, 4, r), F32),
            dma((SLOTS,)),
            dma((EXCHANGES,)), dma((EXCHANGES,)), dma((EXCHANGES,)), dma((EXCHANGES,)),
            dma((REDUCES,)), dma((REDUCES,)), dma((REDUCES,)), dma((REDUCES,)),
            dma((ITERS,)), dma((ITERS,)),
        ]
        return pl.pallas_call(
            functools.partial(entry, nx, ny, (7 + len(fixed),)),
            out_shape=(
                jax.ShapeDtypeStruct((slab, r), F32),
                jax.ShapeDtypeStruct((nc, r), F32),
            ),
            in_specs=[
                pl.BlockSpec(memory_space=pltpu.SMEM),
                pl.BlockSpec(memory_space=pl.ANY),
                vmem, vmem, vmem,
            ],
            out_specs=(vmem, vmem),
            scratch_shapes=fixed + pieces() + pieces() + pieces() + rest,
            compiler_params=pltpu.CompilerParams(
                collective_id=0, has_side_effects=True, vmem_limit_bytes=60 * 1024 * 1024
            ),
            name="projected_cg",
        )(offsets, schur_blocks[0], right_side, coarse_basis, coarse_load)

    in_specs = (
        P(("gx", "gy"), None, None),
        P(("gx", "gy")),
        P(("gx", "gy"), None),
        P(("gx", "gy"), None),
        P(),
    )
    out_specs = (P(("gx", "gy"), None), P())
    return jax.shard_map(local, mesh=mesh, in_specs=in_specs, out_specs=out_specs, check_vma=False)
```

profile of v0, /device:TPU:0, one launch (start us, length us, event | category | flops | bytes accessed | tf_op | source)
XLA Modules:
  0.0 143.2 jit_solution(14047215585919979602)
XLA Ops:
  1.3 138.6 %projected_cg.1 = (f32[1024,128]{1,0:T(8,128)}, f32[128,128]{1,0:T(8,128)}) custom-call(s32[1]{0:T(128)S(6)} %copy.9.refs_0_, f32[2048,2048]{1,0:T(8,128)} %bitcast.1, f32[1024,128]{1,0:T(8,128)} %refs_2_.1, f32[1024,128]{1,0:T(8,128)} %refs_3_.1, f32[128,128]{1,0:T(8,128)} %refs_4_.1), custom_call_target="tpu_custom_call" | custom-call | tf_op jit(solution)/shard_map/projected_cg/pallas_call | solution.py:424
  139.8 1.9 %copy.10 = f32[1024,128]{1,0:T(8,128)} copy(f32[1024,128]{1,0:T(8,128)} %get-tuple-element.4) | data formatting | bytes 1048576
  141.7 1.5 %copy.11 = f32[128,128]{1,0:T(8,128)} copy(f32[128,128]{1,0:T(8,128)} %get-tuple-element.5) | data formatting | bytes 131072
where the time goes:
time: 144 us; the launch traced here: 143 us
  Pallas kernels  139 us (97%)
  local copies, waits for them, and re-layouts  3.34 us (2%)
    pallas_call x1, Pallas kernels, local(): pl.pallas_call(functools.partial(entry, nx, ny, (7 + len(fixed),)), out_s...  139 us
    unnamed x2, local copies, waits for them, and re-layouts  3.34 us

commit v1 on v0

v1 whole, which is shorter than its diff:
```python
import functools

import jax
import jax.numpy as jnp
from jax import lax
from jax.experimental import pallas as pl
from jax.experimental.pallas import tpu as pltpu
from jax.sharding import PartitionSpec as P

ITERS = 3
MESH = pl.DeviceIdType.MESH
HIGHEST = lax.Precision.HIGHEST
F32 = jnp.float32
BF16 = jnp.bfloat16
LANES = 128
CHUNK = 128
SLOTS = 4
BLOCK = 512
EXCHANGES = 3 + 2 * (ITERS - 1)
PARTS = ITERS
IMAGES = ITERS
REDUCES = 2 + ITERS
STEPS = ((1,), (2,), (0, 3))


def dot(a, b):
    return jnp.dot(a, b, precision=HIGHEST, preferred_element_type=F32)


def halves(x):
    hi = x.astype(BF16)
    return hi, (x - hi.astype(F32)).astype(BF16)


def narrow(x):
    return jnp.concatenate(halves(x), axis=1)


def right_operand(x):
    hi, lo = halves(x)
    return jnp.concatenate(
        [jnp.concatenate([hi, lo], axis=1), jnp.concatenate([hi, jnp.zeros_like(lo)], axis=1)], axis=0
    )


def small(left, right):
    both = jnp.dot(left, right, preferred_element_type=F32)
    half = both.shape[1] // 2
    return both[:, :half] + both[:, half:]


def kernel(nx, ny, off_ref, schur_ref, right_hbm, basis_hbm, load_hbm, lam_hbm, amp_hbm, s):
    n = nx * ny
    slab, nc = s["right"].shape
    width = 2 * slab
    low = slab // 4
    span = slab - low
    ix, iy = lax.axis_index("gx"), lax.axis_index("gy")
    me = ix * ny + iy
    off = off_ref[0]
    chunks = width // CHUNK
    tiles = width // LANES
    stages = [s["stage%d" % i] for i in range(SLOTS)]
    s_hi, s_lo, vec, twice = s["s_hi"], s["s_lo"], s["vec"], s["twice"]
    in_l, in_r, out_l, out_r, img = s["in_l"], s["in_r"], s["out_l"], s["out_r"], s["img"]
    right, basis_own, load = s["right"], s["basis_own"], s["load"]
    basis_w, basis_hl, sc, sc_hl = s["basis_w"], s["basis_hl"], s["sc"], s["sc_hl"]
    p_ref, z, base, zbase, si = s["p"], s["z"], s["base"], s["zbase"], s["si"]
    lam, amp_out, d = s["lam"], s["amp"], s["d"]
    m_ref, sweep = s["m"], s["sweep"]
    scal_in, scal_mid, scal_x, scal_y = s["scal_in"], s["scal_mid"], s["scal_x"], s["scal_y"]

    def where_is(i):
        return (lax.div(i, ny), lax.rem(i, ny))

    def fetch(i, slot):
        return pltpu.make_async_copy(
            schur_ref.at[pl.ds(i * CHUNK, CHUNK), :], stages[slot], s["stage_sem"].at[slot]
        )

    def load_in(k):
        src, dst = ((basis_hbm, basis_own), (right_hbm, right), (load_hbm, load))[k]
        return pltpu.make_async_copy(src, dst, s["load_sem"].at[k])

    load_in(0).start()
    barrier = pltpu.get_barrier_semaphore()

    def greet(x, y):
        pl.semaphore_signal(barrier, inc=1, device_id=(x, y), device_id_type=MESH)

    def greet_x(k, carry):
        greet(lax.rem(ix + k, nx), iy)
        return carry

    def greet_y(k, carry):
        greet(ix, lax.rem(iy + k, ny))
        return carry

    turns_left = jnp.logical_and(iy == 0, ix > 0)
    turns_right = jnp.logical_and(iy == ny - 1, ix < nx - 1)

    lax.fori_loop(1, nx, greet_x, 0)
    lax.fori_loop(1, ny, greet_y, 0)

    @pl.when(turns_left)
    def _():
        greet(ix - 1, ny - 1)

    @pl.when(turns_right)
    def _():
        greet(ix + 1, 0)

    load_in(1).start()
    for i in range(SLOTS):
        fetch(i, i).start()
    load_in(2).start()

    @pl.when(me == 0)
    def _():
        in_l[...] = jnp.zeros_like(in_l)

    @pl.when(me == n - 1)
    def _():
        in_r[...] = jnp.zeros_like(in_r)

    def to_right(e, i, src):
        return pltpu.make_async_remote_copy(
            src_ref=src, dst_ref=in_l.at[e, pl.ds(i * low, low)], send_sem=s["hs_r"].at[e, i],
            recv_sem=s["hr_l"].at[e, i], device_id=where_is(lax.rem(me + 1, n)), device_id_type=MESH,
        )

    def to_left(e, i, src):
        return pltpu.make_async_remote_copy(
            src_ref=src, dst_ref=in_r.at[e, pl.ds(i * low, low)], send_sem=s["hs_l"].at[e, i],
            recv_sem=s["hr_r"].at[e, i], device_id=where_is(lax.rem(me + n - 1, n)), device_id_type=MESH,
        )

    any_part = out_l.at[0, pl.ds(0, low)]

    def send(e, i_right, src_right, i_left, src_left):
        if src_left is not None:
            @pl.when(me > 0)
            def _():
                to_left(e, i_left, src_left).start()

        if src_right is not None:
            @pl.when(me < n - 1)
            def _():
                to_right(e, i_right, src_right).start()

    def from_left(e, i):
        @pl.when(me > 0)
        def _():
            to_right(e, i, any_part).wait_recv()

        return in_l[e, i * low : (i + 1) * low, :]

    def from_right(e, i):
        @pl.when(me < n - 1)
        def _():
            to_left(e, i, any_part).wait_recv()

        return in_r[e, i * low : (i + 1) * low, :]

    def below(c):
        return lax.broadcasted_iota(jnp.int32, (low, nc), 0) + c * low < off

    def q(c):
        return slice(c * low, (c + 1) * low)

    def own_q(c):
        return slice(slab + c * low, slab + (c + 1) * low)

    def send_own(e, c, ref):
        view = ref.at[pl.ds(c * low, low)]
        send(e, c - 1, view if c > 0 else None, c, view if c < 3 else None)

    def halo(e, c):
        if c == 0:
            return from_right(e, 0)
        if c == 3:
            return from_left(e, 2)
        left = from_left(e, c - 1)
        return jnp.where(below(c), from_right(e, c), left)

    def send_parts(e, k, c, head):
        mask = below(c)
        if c < 3:
            out_r[k, q(c), :] = jnp.where(mask, head, 0.0) if c > 0 else head
        if c > 0:
            out_l[k, q(c - 1), :] = jnp.where(mask, 0.0, head) if c < 3 else head
        send(
            e,
            c, out_r.at[k, pl.ds(c * low, low)] if c < 3 else None,
            c - 1, out_l.at[k, pl.ds((c - 1) * low, low)] if c > 0 else None,
        )

    def add_parts(e, c, mine):
        if c < 3:
            mine = mine + from_left(e, c)
        if c > 0:
            mine = mine + from_right(e, c - 1)
        return mine

    def put(rows, value):
        hi, lo = halves(value)
        vec[rows, :nc] = hi
        vec[rows, nc:] = lo

    def mul(pieces, first=False, last=False):
        def rows(i, carry):
            at = pl.ds(pl.multiple_of(i * BLOCK, BLOCK), BLOCK)
            acc = None if first else twice[at, :]
            for k0, k1 in pieces:
                both = jnp.dot(s_hi[at, k0:k1], vec[k0:k1, :], preferred_element_type=F32)
                rest = jnp.dot(s_lo[at, k0:k1], vec[k0:k1, :nc], preferred_element_type=F32)
                part = both[:, :nc] + (both[:, nc:] + rest)
                acc = part if acc is None else acc + part
            twice[at, :] = acc
            if last:
                twice[pl.ds(pl.multiple_of(width + i * BLOCK, BLOCK), BLOCK), :] = acc
            return carry

        lax.fori_loop(0, width // BLOCK, rows, 0)

    def mul_quarters(cs, last=False):
        mul([(c * low, (c + 1) * low) for c in cs], last=last)

    def folded(first, count):
        return twice[pl.ds(width - off + first, count), :]

    def x_send(src, dst, sends, recvs):
        for k in range(1, nx):
            peer = lax.rem(ix + k, nx)
            pltpu.make_async_remote_copy(
                src_ref=src(peer), dst_ref=dst, send_sem=sends, recv_sem=recvs,
                device_id=(peer, iy), device_id_type=MESH,
            ).start()

    def y_send(src, dst, sends, recvs):
        def go(k, carry):
            peer = lax.rem(iy + k, ny)
            pltpu.make_async_remote_copy(
                src_ref=src(peer), dst_ref=dst, send_sem=sends, recv_sem=recvs,
                device_id=(ix, peer), device_id_type=MESH,
            ).start()
            return carry

        lax.fori_loop(1, ny, go, 0)

    def wait_for(ref, count, sem):
        view = ref.at[pl.ds(0, count)]
        pltpu.make_async_copy(view, view, sem).wait()

    def red(r):
        return [s[name + str(r)] for name in ("pa", "fa", "pb", "fb", "ga", "gb")]

    def red1(r, value):
        pa, fa = red(r)[:2]
        h = value.shape[0] // nx
        for i in range(nx):
            pa[i] = value[i * h : (i + 1) * h]
        x_send(lambda peer: pa.at[peer], fa.at[ix], s["rs"].at[r, 0], s["rr"].at[r, 0])
        fa[ix] = pa[ix]

    def red2(r):
        _, fa, pb, fb = red(r)[:4]
        wait_for(fa, nx - 1, s["rr"].at[r, 0])
        total = jnp.sum(fa[...], axis=0)
        h = total.shape[0] // ny
        for i in range(ny):
            pb[i] = total[i * h : (i + 1) * h]
        y_send(lambda peer: pb.at[peer], fb.at[iy], s["rs"].at[r, 1], s["rr"].at[r, 1])
        fb[iy] = pb[iy]

    def red3(r):
        fb, ga = red(r)[3:5]
        wait_for(fb, ny - 1, s["rr"].at[r, 1])
        ga[iy] = jnp.sum(fb[...], axis=0)
        y_send(lambda peer: ga.at[iy], ga.at[iy], s["rs"].at[r, 2], s["rr"].at[r, 2])

    def red4(r):
        ga, gb = red(r)[4:]
        wait_for(ga, ny - 1, s["rr"].at[r, 2])
        x_send(lambda peer: ga, gb.at[ix], s["rs"].at[r, 3], s["rr"].at[r, 3])
        gb[ix] = ga[...]

    def red5(r):
        gb = red(r)[5]
        wait_for(gb, nx - 1, s["rr"].at[r, 3])
        h = gb.shape[2]
        for i in range(nx):
            for j in range(ny):
                m_ref[(i * ny + j) * h : (i * ny + j + 1) * h, :] = gb[i, j]
        return m_ref[: n * h, :]

    def scal1(it):
        x_send(lambda peer: scal_in.at[it], scal_x.at[it, ix], s["ss"].at[it, 0], s["sr"].at[it, 0])
        scal_x[it, ix] = scal_in[it]

    def scal2(it):
        wait_for(scal_x.at[it], nx - 1, s["sr"].at[it, 0])
        scal_mid[it] = jnp.sum(scal_x[it], axis=0)
        y_send(lambda peer: scal_mid.at[it], scal_y.at[it, iy], s["ss"].at[it, 1], s["sr"].at[it, 1])
        scal_y[it, iy] = scal_mid[it]

    def scal3(it):
        wait_for(scal_y.at[it], ny - 1, s["sr"].at[it, 1])
        sums = jnp.sum(scal_y[it], axis=0)
        return sums[0:1], sums[1:2], sums[2:3]

    turn, twist = lax.div(off, LANES), lax.rem(off, LANES)
    wraps = lax.broadcasted_iota(jnp.int32, (CHUNK, LANES), 1) < twist

    def split(g, carry):
        for slot in range(SLOTS):
            i = g * SLOTS + slot
            fetch(i, slot).wait()
            at = pl.ds(pl.multiple_of(i * CHUNK, CHUNK), CHUNK)

            def rolled(j):
                m = lax.rem(j - turn + tiles, tiles) * LANES
                return pltpu.roll(stages[slot][:, pl.ds(m, LANES)], twist, 1)

            before = rolled(-1)
            for j in range(tiles):
                now = rolled(j)
                hi, lo = halves(jnp.where(wraps, before, now))
                s_hi[at, j * LANES : (j + 1) * LANES] = hi
                s_lo[at, j * LANES : (j + 1) * LANES] = lo
                before = now

            @pl.when(i + SLOTS < chunks)
            def _():
                fetch(i + SLOTS, slot).start()

        return carry

    groups = chunks // SLOTS

    load_in(0).wait()
    corners = jnp.where(turns_left, 1, 0) + jnp.where(turns_right, 1, 0)
    pl.semaphore_wait(barrier, nx + ny - 2 + corners)

    send_own(0, 1, basis_own)
    load_in(1).wait()
    own_t = basis_own[...].T
    both = dot(own_t, jnp.concatenate([basis_own[...], right[...]], axis=1))
    red1(0, both[:, :nc])
    m_ref[nc:, :] = both[:, nc:]
    lax.fori_loop(0, groups // 4, split, 0)
    send_own(0, 2, basis_own)
    lax.fori_loop(groups // 4, groups // 2, split, 0)
    red2(0)
    for c in STEPS[2]:
        send_own(0, c, basis_own)
    lax.fori_loop(groups // 2, groups, split, 0)
    basis_w[slab:, :] = basis_own[...]
    put(slice(slab, width), basis_own[...])
    mul([(slab, width)], first=True)
    red3(0)
    for step, cs in enumerate(STEPS):
        for c in cs:
            value = halo(0, c)
            basis_w[q(c), :] = value
            put(q(c), value)
        mul_quarters(cs, last=step == 2)
    basis_hl[...] = vec[...]

    for cs in STEPS[:2]:
        for c in cs:
            head = folded(c * low, low)
            send_parts(1, 0, c, head)
            sc[q(c), :] = head
    for c in STEPS[2]:
        head = folded(c * low, low)
        send_parts(1, 0, c, head)
        sc[q(c), :] = head
    sc[slab:, :] = folded(slab, slab)
    red4(0)
    red1(1, jnp.concatenate([dot(basis_w[...].T, sc[...]), m_ref[nc:, :]], axis=0))
    sweep[...] = red5(0)
    sc_hl[:, :nc] = sc[...].astype(BF16)
    sc_hl[:, nc:] = (sc[...] - sc[...].astype(BF16).astype(F32)).astype(BF16)
    red2(1)

    lanes = lax.broadcasted_iota(jnp.int32, (nc, nc), 1)
    subs = lax.broadcasted_iota(jnp.int32, (nc, nc), 0)

    def eliminate(a, k, row, col, p):
        here = lanes == k
        inverse = 1.0 / p
        scaled = row * inverse
        new = a - col * scaled
        new = jnp.where(here, col * inverse, new)
        return jnp.where(subs == k, jnp.where(here, -inverse, scaled), new), scaled, inverse

    def pick(row, k):
        return jnp.sum(jnp.where(lanes[:1] == k, row, 0.0), axis=1, keepdims=True)

    def pivot(half, a):
        k = 2 * half
        row1, row2 = sweep[pl.ds(k, 1), :], sweep[pl.ds(k + 1, 1), :]
        col1 = jnp.sum(jnp.where(lanes == k, a, 0.0), axis=1, keepdims=True)
        col2 = jnp.sum(jnp.where(lanes == k + 1, a, 0.0), axis=1, keepdims=True)
        p1, cross, p2 = pick(row1, k), pick(row1, k + 1), pick(row2, k + 1)
        a, scaled, inverse = eliminate(a, k, row1, col1, p1)
        ratio = cross * inverse
        row2 = jnp.where(lanes[:1] == k, ratio, row2 - cross * scaled)
        col2 = jnp.where(subs[:, :1] == k, ratio, col2 - col1 * ratio)
        a, _, _ = eliminate(a, k + 1, row2, col2, p2 - cross * ratio)
        sweep[...] = a
        return a

    ginv = -lax.fori_loop(0, nc // 2, pivot, sweep[...])
    red3(1)
    load_in(2).wait()
    y0 = dot(ginv, load[...])
    y0_op = right_operand(y0)

    fc = s["fc"]
    for cs in STEPS:
        for c in cs:
            fc_c = add_parts(1, c, sc[own_q(c), :])
            fc[q(c), :] = fc_c
            img[0, own_q(c), :] = right[q(c), :] - small(narrow(fc_c), y0_op)
            send_own(2, c, img.at[0, pl.ds(slab, slab)])
    put(slice(slab, width), img[0, slab:, :])
    mul([(slab, width)], first=True)
    red4(1)
    lam[...] = small(basis_hl[slab:, :], y0_op)
    fc_hi, fc_lo = halves(fc[...].T)
    s["fct_hi"][...] = fc_hi
    s["fct_lo"][...] = fc_lo

    def coarse(rows):
        both = jnp.dot(s["fct_hi"][...], rows, preferred_element_type=F32)
        rest = jnp.dot(s["fct_lo"][...], rows[:, :nc], preferred_element_type=F32)
        return both[:, :nc] + (both[:, nc:] + rest)

    sums = red5(1)
    amp = dot(ginv, sums[nc:] - dot(sums[:nc], y0))

    def bases(op, step, beta, old):
        def rows(i, carry):
            at = pl.ds(pl.multiple_of(i * BLOCK, BLOCK), BLOCK)
            cs = small(basis_hl[at, :], op)
            ss = small(sc_hl[at, :], op)
            if step is None:
                zbase[at, :] = -cs
                base[at, :] = -ss
            elif beta is None:
                zbase[at, :] = z[at, :] + step * cs
                base[at, :] = p_ref[at, :] + step * ss
            else:
                zbase[at, :] = z[at, :] + step * (cs - beta * img[old, at, :])
                base[at, :] = p_ref[at, :] + step * (ss - beta * si[at, :])
            return carry

        lax.fori_loop(0, width // BLOCK, rows, 0)

    bases(right_operand(amp), None, None, None)
    z[slab:, :] = zbase[slab:, :] + img[0, slab:, :]
    red1(2, coarse(narrow(z[slab:, :])))

    energy = curvature = coarse_image = step = beta = None
    for it in range(ITERS):
        last = it == ITERS - 1
        e = 2 + 2 * it
        scale = 1.0 if it == 0 else -step
        r = 2 + it

        for k, cs in enumerate(STEPS):
            for c in cs:
                value = halo(e, c)
                img[it, q(c), :] = value
                put(q(c), value)
            mul_quarters(cs, last=k == 2)
            if k == 0:
                red2(r)

        for cs in STEPS[:2]:
            for c in cs:
                p_c = base[q(c), :] + scale * folded(c * low, low)
                p_ref[q(c), :] = p_c
                if not last:
                    send_parts(e + 1, 1 + it, c, p_c)
        for c in STEPS[2]:
            p_ref[q(c), :] = base[q(c), :] + scale * folded(c * low, low)
        if it == 1:
            pass
        p_ref[slab:, :] = base[slab:, :] + scale * folded(slab, slab)
        z[:slab, :] = zbase[:slab, :] + scale * img[it, :slab, :]
        scal_in[it, 0:1] = jnp.sum(z[...] * p_ref[...], axis=0, keepdims=True)
        scal_in[it, 1:2] = jnp.sum(z[slab:, :] * z[slab:, :], axis=0, keepdims=True)
        if it == 0:
            scal_in[it, 2:3] = jnp.zeros((1, nc), F32)
        else:
            own = img[it, slab:, :]
            if it > 1:
                own = own + beta * s["image"][...]
            s["image"][...] = own
            scal_in[it, 2:3] = jnp.sum(z[slab:, :] * own, axis=0, keepdims=True)
        scal_in[it, 3:4] = jnp.zeros((1, nc), F32)
        scal1(it)
        if it > 0 and not last:
            raw = folded(0, width)
            si[...] = raw if it == 1 else raw + beta * si[...]
        red3(r)
        scal2(it)
        if not last:
            for c in STEPS[2]:
                send_parts(e + 1, 1 + it, c, p_ref[q(c), :])
            for cs in STEPS[:2]:
                for c in cs:
                    img[it + 1, own_q(c), :] = add_parts(e + 1, c, p_ref[own_q(c), :])
                    send_own(e + 2, c, img.at[it + 1, pl.ds(slab, slab)])
        red4(r)
        curved, energy_now, crossed = scal3(it)
        if not last:
            for c in STEPS[2]:
                img[it + 1, own_q(c), :] = add_parts(e + 1, c, p_ref[own_q(c), :])
                send_own(e + 2, c, img.at[it + 1, pl.ds(slab, slab)])
            put(slice(slab, width), img[it + 1, slab:, :])
            mul([(slab, width)], first=True)
        coarse_now = red5(r)
        if it == 0:
            d[...] = z[slab:, :]
            curvature = curved
            coarse_image = coarse_now
        else:
            beta = energy_now / energy
            d[...] = z[slab:, :] + beta * d[...]
            curvature = curved + beta * (2.0 * crossed + beta * curvature)
            coarse_image = coarse_now + beta * coarse_image
        energy = energy_now
        step = energy / curvature
        lam[...] += step * d[...]
        shift = dot(ginv, coarse_image)
        amp = amp - step * shift
        if not last:
            bases(right_operand(shift), step, beta, it)
            z[slab:, :] = zbase[slab:, :] - step * img[it + 1, slab:, :]
            red1(r + 1, coarse(narrow(z[slab:, :])))

    amp_out[...] = amp
    out_lam = pltpu.make_async_copy(lam, lam_hbm, s["load_sem"].at[0])
    out_amp = pltpu.make_async_copy(amp_out, amp_hbm, s["load_sem"].at[1])
    out_lam.start()
    out_amp.start()

    for e in range(EXCHANGES):
        for i in range(3):
            @pl.when(me > 0)
            def _():
                to_left(e, i, any_part).wait_send()

            @pl.when(me < n - 1)
            def _():
                to_right(e, i, any_part).wait_send()

    for r in range(REDUCES):
        pa, _, pb, _, ga, gb = red(r)
        wait_for(pa, nx - 1, s["rs"].at[r, 0])
        wait_for(pb, ny - 1, s["rs"].at[r, 1])
        wait_for(ga, ny - 1, s["rs"].at[r, 2])
        wait_for(gb, nx - 1, s["rs"].at[r, 3])
    for it in range(ITERS):
        wait_for(scal_x.at[it], nx - 1, s["ss"].at[it, 0])
        wait_for(scal_y.at[it], ny - 1, s["ss"].at[it, 1])
    out_lam.wait()
    out_amp.wait()


def entry(nx, ny, names, *refs):
    fixed = len(refs) - len(names)
    kernel(nx, ny, *refs[:fixed], dict(zip(names, refs[fixed:])))


def solution(mesh):
    nx, ny = mesh.shape["gx"], mesh.shape["gy"]

    def local(schur_blocks, offsets, right_side, coarse_basis, coarse_load):
        slab, r = right_side.shape
        nc = coarse_basis.shape[1]
        width = schur_blocks.shape[1]
        span = slab - slab // 4
        vmem, dma = pltpu.VMEM, pltpu.SemaphoreType.DMA
        scratch = {"stage%d" % i: vmem((CHUNK, width), F32) for i in range(SLOTS)}
        scratch |= {name: vmem((width, width), BF16) for name in ("s_hi", "s_lo")}
        scratch |= {name: vmem((width, 2 * nc), BF16) for name in ("vec", "basis_hl", "sc_hl")}
        scratch |= {name: vmem((width, r), F32) for name in ("basis_w", "sc", "p", "z", "base", "zbase", "si")}
        scratch |= {name: vmem((slab, r), F32) for name in ("right", "basis_own", "lam", "d", "fc", "image")}
        scratch |= {name: vmem((nc, r), F32) for name in ("load", "amp", "sweep")}
        scratch |= {name: vmem((nc, slab), BF16) for name in ("fct_hi", "fct_lo")}
        scratch |= {
            "twice": vmem((2 * width, r), F32),
            "img": vmem((IMAGES, width, r), F32),
            "out_l": vmem((PARTS, span, r), F32),
            "out_r": vmem((PARTS, span, r), F32),
            "in_l": vmem((EXCHANGES, span, r), F32),
            "in_r": vmem((EXCHANGES, span, r), F32),
            "m": vmem((2 * nc, r), F32),
            "scal_in": vmem((ITERS, 4, r), F32),
            "scal_mid": vmem((ITERS, 4, r), F32),
            "scal_x": vmem((ITERS, nx, 4, r), F32),
            "scal_y": vmem((ITERS, ny, 4, r), F32),
        }
        for k in range(REDUCES):
            rows = 2 * nc if k == 1 else nc
            h, p = rows // nx, rows // (nx * ny)
            scratch |= {
                "pa%d" % k: vmem((nx, h, r), F32),
                "fa%d" % k: vmem((nx, h, r), F32),
                "pb%d" % k: vmem((ny, p, r), F32),
                "fb%d" % k: vmem((ny, p, r), F32),
                "ga%d" % k: vmem((ny, p, r), F32),
                "gb%d" % k: vmem((nx, ny, p, r), F32),
            }
        scratch |= {name: dma((EXCHANGES, 3)) for name in ("hs_l", "hs_r", "hr_l", "hr_r")}
        scratch |= {
            "stage_sem": dma((SLOTS,)),
            "load_sem": dma((3,)),
            "rs": dma((REDUCES, 4)),
            "rr": dma((REDUCES, 4)),
            "ss": dma((ITERS, 2)),
            "sr": dma((ITERS, 2)),
        }
        names = tuple(scratch)
        hbm = pl.BlockSpec(memory_space=pl.ANY)
        return pl.pallas_call(
            functools.partial(entry, nx, ny, names),
            out_shape=(
                jax.ShapeDtypeStruct((slab, r), F32),
                jax.ShapeDtypeStruct((nc, r), F32),
            ),
            in_specs=[pl.BlockSpec(memory_space=pltpu.SMEM), hbm, hbm, hbm, hbm],
            out_specs=(hbm, hbm),
            scratch_shapes=list(scratch.values()),
            compiler_params=pltpu.CompilerParams(
                collective_id=0, has_side_effects=True, vmem_limit_bytes=60 * 1024 * 1024
            ),
            name="projected_cg",
        )(offsets, schur_blocks[0], right_side, coarse_basis, coarse_load)

    in_specs = (
        P(("gx", "gy"), None, None),
        P(("gx", "gy")),
        P(("gx", "gy"), None),
        P(("gx", "gy"), None),
        P(),
    )
    out_specs = (P(("gx", "gy"), None), P())
    return jax.shard_map(local, mesh=mesh, in_specs=in_specs, out_specs=out_specs, check_vma=False)
```

time: 144 us -> 115 us (0.80)
  Pallas kernels: 139 us -> 110 us
    pallas_call x1, Pallas kernels: 139 us -> 110 us  [local(): pl.pallas_call(functools.partial(entry, nx, ny, names), out_shape=(jax.Sh...]
where the time goes in v1:
time: 115 us
  Pallas kernels  110 us (96%)
  local copies, waits for them, and re-layouts  3.34 us (3%)
  between operations  1.29 us (1%)
    pallas_call x1, Pallas kernels, local(): pl.pallas_call(functools.partial(entry, nx, ny, names), out_shape=(jax.Sh...  110 us
    unnamed x2, local copies, waits for them, and re-layouts  3.34 us

profile of v1, /device:TPU:0, one launch (start us, length us, event | category | flops | bytes accessed | tf_op | source)
XLA Modules:
  0.0 114.6 jit_solution(7366648954666699441)
XLA Ops:
  1.3 110.0 %projected_cg.1 = (f32[1024,128]{1,0:T(8,128)}, f32[128,128]{1,0:T(8,128)}) custom-call(s32[1]{0:T(128)S(6)} %copy.9.refs_0_, f32[2048,2048]{1,0:T(8,128)} %bitcast.1, f32[1024,128]{1,0:T(8,128)} %refs_2_.1, f32[1024,128]{1,0:T(8,128)} %refs_3_.1, f32[128,128]{1,0:T(8,128)} %refs_4_.1), custom_call_target="tpu_custom_call" | custom-call | tf_op jit(solution)/shard_map/projected_cg/pallas_call | solution.py:631
  111.2 1.9 %copy.10 = f32[1024,128]{1,0:T(8,128)} copy(f32[1024,128]{1,0:T(8,128)} %get-tuple-element.4) | data formatting | bytes 1048576
  113.1 1.5 %copy.11 = f32[128,128]{1,0:T(8,128)} copy(f32[128,128]{1,0:T(8,128)} %get-tuple-element.5) | data formatting | bytes 131072

commit v2 on v1

--- a/solution.py
+++ b/solution.py
@@ -14,12 +14,14 @@
 BF16 = jnp.bfloat16
 LANES = 128
 CHUNK = 128
-SLOTS = 4
+SLOTS = 2
+GROUP = 512
 BLOCK = 512
+PIVOTS = 4
 EXCHANGES = 3 + 2 * (ITERS - 1)
 PARTS = ITERS
 IMAGES = ITERS
-REDUCES = 2 + ITERS
+REDUCES = 1 + ITERS
 STEPS = ((1,), (2,), (0, 3))
 
 
@@ -58,13 +60,13 @@
     ix, iy = lax.axis_index("gx"), lax.axis_index("gy")
     me = ix * ny + iy
     off = off_ref[0]
-    chunks = width // CHUNK
+    groups = width // GROUP
     tiles = width // LANES
     stages = [s["stage%d" % i] for i in range(SLOTS)]
     s_hi, s_lo, vec, twice = s["s_hi"], s["s_lo"], s["vec"], s["twice"]
     in_l, in_r, out_l, out_r, img = s["in_l"], s["in_r"], s["out_l"], s["out_r"], s["img"]
     right, basis_own, load = s["right"], s["basis_own"], s["load"]
-    basis_w, basis_hl, sc, sc_hl = s["basis_w"], s["basis_hl"], s["sc"], s["sc_hl"]
+    basis_hl, sc, sc_hl = s["basis_hl"], s["sc"], s["sc_hl"]
     p_ref, z, base, zbase, si = s["p"], s["z"], s["base"], s["zbase"], s["si"]
     lam, amp_out, d = s["lam"], s["amp"], s["d"]
     m_ref, sweep = s["m"], s["sweep"]
@@ -75,7 +77,7 @@
 
     def fetch(i, slot):
         return pltpu.make_async_copy(
-            schur_ref.at[pl.ds(i * CHUNK, CHUNK), :], stages[slot], s["stage_sem"].at[slot]
+            schur_ref.at[pl.ds(i * GROUP, GROUP), :], stages[slot], s["stage_sem"].at[slot]
         )
 
     def load_in(k):
@@ -207,21 +209,29 @@
         vec[rows, :nc] = hi
         vec[rows, nc:] = lo
 
+    def product(at, pieces):
+        total = None
+        for k0, k1 in pieces:
+            both = jnp.dot(s_hi[at, k0:k1], vec[k0:k1, :], preferred_element_type=F32)
+            rest = jnp.dot(s_lo[at, k0:k1], vec[k0:k1, :nc], preferred_element_type=F32)
+            part = both[:, :nc] + (both[:, nc:] + rest)
+            total = part if total is None else total + part
+        return total
+
     def mul(pieces, first=False, last=False):
+        tall = width if not first else slab
+
         def rows(i, carry):
-            at = pl.ds(pl.multiple_of(i * BLOCK, BLOCK), BLOCK)
-            acc = None if first else twice[at, :]
-            for k0, k1 in pieces:
-                both = jnp.dot(s_hi[at, k0:k1], vec[k0:k1, :], preferred_element_type=F32)
-                rest = jnp.dot(s_lo[at, k0:k1], vec[k0:k1, :nc], preferred_element_type=F32)
-                part = both[:, :nc] + (both[:, nc:] + rest)
-                acc = part if acc is None else acc + part
+            at = pl.ds(pl.multiple_of(i * tall, tall), tall)
+            acc = product(at, pieces)
+            if not first:
+                acc = twice[at, :] + acc
             twice[at, :] = acc
             if last:
-                twice[pl.ds(pl.multiple_of(width + i * BLOCK, BLOCK), BLOCK), :] = acc
+                twice[pl.ds(pl.multiple_of(width + i * tall, tall), tall), :] = acc
             return carry
 
-        lax.fori_loop(0, width // BLOCK, rows, 0)
+        lax.fori_loop(0, width // tall, rows, 0)
 
     def mul_quarters(cs, last=False):
         mul([(c * low, (c + 1) * low) for c in cs], last=last)
@@ -295,32 +305,72 @@
         return m_ref[: n * h, :]
 
     def scal1(it):
-        x_send(lambda peer: scal_in.at[it], scal_x.at[it, ix], s["ss"].at[it, 0], s["sr"].at[it, 0])
-        scal_x[it, ix] = scal_in[it]
+        y_send(lambda peer: scal_in.at[it], scal_y.at[it, iy], s["ss"].at[it, 1], s["sr"].at[it, 1])
+        scal_y[it, iy] = scal_in[it]
 
     def scal2(it):
+        wait_for(scal_y.at[it], ny - 1, s["sr"].at[it, 1])
+        scal_mid[it] = jnp.sum(scal_y[it], axis=0)
+        x_send(lambda peer: scal_mid.at[it], scal_x.at[it, ix], s["ss"].at[it, 0], s["sr"].at[it, 0])
+        scal_x[it, ix] = scal_mid[it]
+
+    def scal3(it):
         wait_for(scal_x.at[it], nx - 1, s["sr"].at[it, 0])
-        scal_mid[it] = jnp.sum(scal_x[it], axis=0)
-        y_send(lambda peer: scal_mid.at[it], scal_y.at[it, iy], s["ss"].at[it, 1], s["sr"].at[it, 1])
-        scal_y[it, iy] = scal_mid[it]
-
-    def scal3(it):
-        wait_for(scal_y.at[it], ny - 1, s["sr"].at[it, 1])
-        sums = jnp.sum(scal_y[it], axis=0)
+        sums = jnp.sum(scal_x[it], axis=0)
         return sums[0:1], sums[1:2], sums[2:3]
+
+    def scal_all(it):
+        all_send(lambda peer: scal_in.at[it], s["scal_a"].at[me], s["ss"].at[it, 0], s["sr"].at[it, 0])
+        s["scal_a"][me] = scal_in[it]
+
+    def scal_sum(it):
+        wait_for(s["scal_a"], n - 1, s["sr"].at[it, 0])
+        sums = jnp.sum(s["scal_a"][...], axis=0)
+        return sums[0:1], sums[1:2], sums[2:3]
+
+    def all_send(src, dst, sends, recvs):
+        def go(k, carry):
+            peer = lax.rem(me + k, n)
+            pltpu.make_async_remote_copy(
+                src_ref=src(peer), dst_ref=dst, send_sem=sends, recv_sem=recvs,
+                device_id=where_is(peer), device_id_type=MESH,
+            ).start()
+            return carry
+
+        lax.fori_loop(1, n, go, 0)
+
+    def direct1(value):
+        h = value.shape[0] // n
+        for i in range(n):
+            s["dp"][i] = value[i * h : (i + 1) * h]
+        all_send(lambda peer: s["dp"].at[peer], s["df"].at[me], s["ds"].at[0], s["dr"].at[0])
+        s["df"][me] = s["dp"][me]
+
+    def direct2():
+        wait_for(s["df"], n - 1, s["dr"].at[0])
+        s["dt"][me] = jnp.sum(s["df"][...], axis=0)
+        all_send(lambda peer: s["dt"].at[me], s["dt"].at[me], s["ds"].at[1], s["dr"].at[1])
+
+    def direct3():
+        wait_for(s["dt"], n - 1, s["dr"].at[1])
+        h = s["dt"].shape[1]
+        for i in range(n):
+            m_ref[i * h : (i + 1) * h, :] = s["dt"][i]
+        return m_ref[: n * h, :]
 
     turn, twist = lax.div(off, LANES), lax.rem(off, LANES)
     wraps = lax.broadcasted_iota(jnp.int32, (CHUNK, LANES), 1) < twist
 
-    def split(g, carry):
-        for slot in range(SLOTS):
-            i = g * SLOTS + slot
-            fetch(i, slot).wait()
-            at = pl.ds(pl.multiple_of(i * CHUNK, CHUNK), CHUNK)
+    def split(g):
+        slot = g % SLOTS
+        fetch(g, slot).wait()
+        for i in range(GROUP // CHUNK):
+            rows = slice(i * CHUNK, (i + 1) * CHUNK)
+            at = slice(g * GROUP + i * CHUNK, g * GROUP + (i + 1) * CHUNK)
 
             def rolled(j):
                 m = lax.rem(j - turn + tiles, tiles) * LANES
-                return pltpu.roll(stages[slot][:, pl.ds(m, LANES)], twist, 1)
+                return pltpu.roll(stages[slot][rows, pl.ds(m, LANES)], twist, 1)
 
             before = rolled(-1)
             for j in range(tiles):
@@ -329,42 +379,50 @@
                 s_hi[at, j * LANES : (j + 1) * LANES] = hi
                 s_lo[at, j * LANES : (j + 1) * LANES] = lo
                 before = now
-
-            @pl.when(i + SLOTS < chunks)
-            def _():
-                fetch(i + SLOTS, slot).start()
-
-        return carry
-
-    groups = chunks // SLOTS
+        if g + SLOTS < groups:
+            fetch(g + SLOTS, slot).start()
+
+    def mul_group(g):
+        at = slice(g * GROUP, (g + 1) * GROUP)
+        twice[at, :] = product(at, [(slab, width)])
 
     load_in(0).wait()
-    corners = jnp.where(turns_left, 1, 0) + jnp.where(turns_right, 1, 0)
-    pl.semaphore_wait(barrier, nx + ny - 2 + corners)
-
-    send_own(0, 1, basis_own)
     load_in(1).wait()
     own_t = basis_own[...].T
     both = dot(own_t, jnp.concatenate([basis_own[...], right[...]], axis=1))
+    m_ref[nc:, :] = both[:, nc:]
+    hi, lo = halves(own_t)
+    s["bt_hi"][:, slab:] = hi
+    s["bt_lo"][:, slab:] = lo
+    put(slice(slab, width), basis_own[...])
+    corners = jnp.where(turns_left, 1, 0) + jnp.where(turns_right, 1, 0)
+    pl.semaphore_wait(barrier, nx + ny - 2 + corners)
+
     red1(0, both[:, :nc])
-    m_ref[nc:, :] = both[:, nc:]
-    lax.fori_loop(0, groups // 4, split, 0)
-    send_own(0, 2, basis_own)
-    lax.fori_loop(groups // 4, groups // 2, split, 0)
+    send_own(0, 1, basis_own)
+    split(0)
+    mul_group(0)
+    split(1)
     red2(0)
+    for c in STEPS[1]:
+        send_own(0, c, basis_own)
+    for g in range(2, groups):
+        mul_group(g - 1)
+        split(g)
+    red3(0)
     for c in STEPS[2]:
         send_own(0, c, basis_own)
-    lax.fori_loop(groups // 2, groups, split, 0)
-    basis_w[slab:, :] = basis_own[...]
-    put(slice(slab, width), basis_own[...])
-    mul([(slab, width)], first=True)
-    red3(0)
+    mul_group(groups - 1)
     for step, cs in enumerate(STEPS):
         for c in cs:
             value = halo(0, c)
-            basis_w[q(c), :] = value
+            hi, lo = halves(value.T)
+            s["bt_hi"][:, q(c)] = hi
+            s["bt_lo"][:, q(c)] = lo
             put(q(c), value)
         mul_quarters(cs, last=step == 2)
+        if step == 1:
+            red4(0)
     basis_hl[...] = vec[...]
 
     for cs in STEPS[:2]:
@@ -377,12 +435,11 @@
         send_parts(1, 0, c, head)
         sc[q(c), :] = head
     sc[slab:, :] = folded(slab, slab)
-    red4(0)
-    red1(1, jnp.concatenate([dot(basis_w[...].T, sc[...]), m_ref[nc:, :]], axis=0))
+    sc_hl[...] = narrow(sc[...])
+    both = jnp.dot(s["bt_hi"][...], sc_hl[...], preferred_element_type=F32)
+    rest = jnp.dot(s["bt_lo"][...], sc_hl[:, :nc], preferred_element_type=F32)
+    red1(1, jnp.concatenate([both[:, :nc] + (both[:, nc:] + rest), m_ref[nc:, :]], axis=0))
     sweep[...] = red5(0)
-    sc_hl[:, :nc] = sc[...].astype(BF16)
-    sc_hl[:, nc:] = (sc[...] - sc[...].astype(BF16).astype(F32)).astype(BF16)
-    red2(1)
 
     lanes = lax.broadcasted_iota(jnp.int32, (nc, nc), 1)
     subs = lax.broadcasted_iota(jnp.int32, (nc, nc), 0)
@@ -398,22 +455,26 @@
     def pick(row, k):
         return jnp.sum(jnp.where(lanes[:1] == k, row, 0.0), axis=1, keepdims=True)
 
-    def pivot(half, a):
-        k = 2 * half
-        row1, row2 = sweep[pl.ds(k, 1), :], sweep[pl.ds(k + 1, 1), :]
-        col1 = jnp.sum(jnp.where(lanes == k, a, 0.0), axis=1, keepdims=True)
-        col2 = jnp.sum(jnp.where(lanes == k + 1, a, 0.0), axis=1, keepdims=True)
-        p1, cross, p2 = pick(row1, k), pick(row1, k + 1), pick(row2, k + 1)
-        a, scaled, inverse = eliminate(a, k, row1, col1, p1)
-        ratio = cross * inverse
-        row2 = jnp.where(lanes[:1] == k, ratio, row2 - cross * scaled)
-        col2 = jnp.where(subs[:, :1] == k, ratio, col2 - col1 * ratio)
-        a, _, _ = eliminate(a, k + 1, row2, col2, p2 - cross * ratio)
+    def pivot(turn, a):
+        k = PIVOTS * turn
+        some = range(PIVOTS)
+        rows = [sweep[pl.ds(k + i, 1), :] for i in some]
+        cols = [jnp.sum(jnp.where(lanes == k + i, a, 0.0), axis=1, keepdims=True) for i in some]
+        block = {(i, j): pick(rows[i], k + j) for i in some for j in some if i <= j}
+        for i in some:
+            a, scaled, inverse = eliminate(a, k + i, rows[i], cols[i], block[i, i])
+            for j in range(i + 1, PIVOTS):
+                ratio = block[i, j] * inverse
+                rows[j] = jnp.where(lanes[:1] == k + i, ratio, rows[j] - block[i, j] * scaled)
+                cols[j] = jnp.where(subs[:, :1] == k + i, ratio, cols[j] - cols[i] * ratio)
+                for l in range(j, PIVOTS):
+                    block[j, l] = block[j, l] - ratio * block[i, l]
         sweep[...] = a
         return a
 
-    ginv = -lax.fori_loop(0, nc // 2, pivot, sweep[...])
-    red3(1)
+    half_way = lax.fori_loop(0, nc // PIVOTS // 2, pivot, sweep[...])
+    red2(1)
+    ginv = -lax.fori_loop(nc // PIVOTS // 2, nc // PIVOTS, pivot, half_way)
     load_in(2).wait()
     y0 = dot(ginv, load[...])
     y0_op = right_operand(y0)
@@ -425,10 +486,8 @@
             fc[q(c), :] = fc_c
             img[0, own_q(c), :] = right[q(c), :] - small(narrow(fc_c), y0_op)
             send_own(2, c, img.at[0, pl.ds(slab, slab)])
-    put(slice(slab, width), img[0, slab:, :])
-    mul([(slab, width)], first=True)
-    red4(1)
-    lam[...] = small(basis_hl[slab:, :], y0_op)
+        if cs == STEPS[0]:
+            red3(1)
     fc_hi, fc_lo = halves(fc[...].T)
     s["fct_hi"][...] = fc_hi
     s["fct_lo"][...] = fc_lo
@@ -438,30 +497,60 @@
         rest = jnp.dot(s["fct_lo"][...], rows[:, :nc], preferred_element_type=F32)
         return both[:, :nc] + (both[:, nc:] + rest)
 
-    sums = red5(1)
-    amp = dot(ginv, sums[nc:] - dot(sums[:nc], y0))
+    red1(2, coarse(narrow(img[0, slab:, :])))
+    put(slice(slab, width), img[0, slab:, :])
+    mul([(slab, width)], first=True)
+    red4(1)
+    red2(2)
+    lam[...] = small(basis_hl[slab:, :], y0_op)
+
+    def own_z(op, step, beta, old):
+        cs = small(basis_hl[slab:, :], op)
+        if step is None:
+            z[slab:, :] = img[old, slab:, :] - cs
+        elif beta is None:
+            z[slab:, :] = z[slab:, :] + step * (cs - img[old + 1, slab:, :])
+        else:
+            z[slab:, :] = z[slab:, :] + step * (cs - beta * img[old, slab:, :] - img[old + 1, slab:, :])
 
     def bases(op, step, beta, old):
         def rows(i, carry):
             at = pl.ds(pl.multiple_of(i * BLOCK, BLOCK), BLOCK)
-            cs = small(basis_hl[at, :], op)
             ss = small(sc_hl[at, :], op)
             if step is None:
-                zbase[at, :] = -cs
                 base[at, :] = -ss
             elif beta is None:
-                zbase[at, :] = z[at, :] + step * cs
                 base[at, :] = p_ref[at, :] + step * ss
             else:
-                zbase[at, :] = z[at, :] + step * (cs - beta * img[old, at, :])
                 base[at, :] = p_ref[at, :] + step * (ss - beta * si[at, :])
             return carry
 
+        def halo_rows(i, carry):
+            at = pl.ds(pl.multiple_of(i * BLOCK, BLOCK), BLOCK)
+            cs = small(basis_hl[at, :], op)
+            if step is None:
+                zbase[at, :] = -cs
+            elif beta is None:
+                zbase[at, :] = z[at, :] + step * cs
+            else:
+                zbase[at, :] = z[at, :] + step * (cs - beta * img[old, at, :])
+            return carry
+
         lax.fori_loop(0, width // BLOCK, rows, 0)
-
-    bases(right_operand(amp), None, None, None)
-    z[slab:, :] = zbase[slab:, :] + img[0, slab:, :]
-    red1(2, coarse(narrow(z[slab:, :])))
+        lax.fori_loop(0, slab // BLOCK, halo_rows, 0)
+
+    def own_scalars(it, beta):
+        mine = z[slab:, :]
+        scal_in[it, 1:2] = jnp.sum(mine * mine, axis=0, keepdims=True)
+        scal_in[it, 3:4] = jnp.zeros((1, nc), F32)
+        if it == 0:
+            scal_in[it, 2:3] = jnp.zeros((1, nc), F32)
+            return
+        image = img[it, slab:, :]
+        if it > 1:
+            image = image + beta * s["image"][...]
+        s["image"][...] = image
+        scal_in[it, 2:3] = jnp.sum(mine * image, axis=0, keepdims=True)
 
     energy = curvature = coarse_image = step = beta = None
     for it in range(ITERS):
@@ -476,72 +565,98 @@
                 img[it, q(c), :] = value
                 put(q(c), value)
             mul_quarters(cs, last=k == 2)
-            if k == 0:
-                red2(r)
-
-        for cs in STEPS[:2]:
-            for c in cs:
-                p_c = base[q(c), :] + scale * folded(c * low, low)
-                p_ref[q(c), :] = p_c
-                if not last:
-                    send_parts(e + 1, 1 + it, c, p_c)
-        for c in STEPS[2]:
+            if k == 0 and it == 0:
+                sums = red5(1)
+                cfc = s["cfc"]
+                cfc[...] = sums[:nc]
+                amp = dot(ginv, sums[nc:] - dot(cfc[...], y0))
+                known = -dot(cfc[...], amp)
+                op = right_operand(amp)
+                own_z(op, None, None, 0)
+                own_scalars(0, None)
+                bases(op, None, None, 0)
+
+        if last:
+            direct2()
+
+        def next_p(c):
+            p_c = base[q(c), :] + scale * folded(c * low, low)
+            p_ref[q(c), :] = p_c
+            if not last:
+                send_parts(e + 1, 1 + it, c, p_c)
+
+        for c in STEPS[0]:
+            next_p(c)
+        for c in STEPS[1] + STEPS[2]:
             p_ref[q(c), :] = base[q(c), :] + scale * folded(c * low, low)
-        if it == 1:
-            pass
         p_ref[slab:, :] = base[slab:, :] + scale * folded(slab, slab)
         z[:slab, :] = zbase[:slab, :] + scale * img[it, :slab, :]
         scal_in[it, 0:1] = jnp.sum(z[...] * p_ref[...], axis=0, keepdims=True)
-        scal_in[it, 1:2] = jnp.sum(z[slab:, :] * z[slab:, :], axis=0, keepdims=True)
-        if it == 0:
-            scal_in[it, 2:3] = jnp.zeros((1, nc), F32)
+        if last:
+            scal_all(it)
         else:
-            own = img[it, slab:, :]
-            if it > 1:
-                own = own + beta * s["image"][...]
-            s["image"][...] = own
-            scal_in[it, 2:3] = jnp.sum(z[slab:, :] * own, axis=0, keepdims=True)
-        scal_in[it, 3:4] = jnp.zeros((1, nc), F32)
-        scal1(it)
+            scal1(it)
+        if not last:
+            red3(r)
+            for c in STEPS[1] + STEPS[2]:
+                send_parts(e + 1, 1 + it, c, p_ref[q(c), :])
         if it > 0 and not last:
             raw = folded(0, width)
             si[...] = raw if it == 1 else raw + beta * si[...]
-        red3(r)
-        scal2(it)
+
+        def next_image(cs):
+            for c in cs:
+                value = add_parts(e + 1, c, p_ref[own_q(c), :])
+                img[it + 1, own_q(c), :] = value
+                send_own(e + 2, c, img.at[it + 1, pl.ds(slab, slab)])
+                put(own_q(c), value)
+
+        def mul_own(cs):
+            mul([(slab + c * low, slab + (c + 1) * low) for c in cs], first=cs == STEPS[0])
+
         if not last:
-            for c in STEPS[2]:
-                send_parts(e + 1, 1 + it, c, p_ref[q(c), :])
-            for cs in STEPS[:2]:
-                for c in cs:
-                    img[it + 1, own_q(c), :] = add_parts(e + 1, c, p_ref[own_q(c), :])
-                    send_own(e + 2, c, img.at[it + 1, pl.ds(slab, slab)])
-        red4(r)
-        curved, energy_now, crossed = scal3(it)
+            next_image(STEPS[0])
+            mul_own(STEPS[0])
         if not last:
-            for c in STEPS[2]:
-                img[it + 1, own_q(c), :] = add_parts(e + 1, c, p_ref[own_q(c), :])
-                send_own(e + 2, c, img.at[it + 1, pl.ds(slab, slab)])
-            put(slice(slab, width), img[it + 1, slab:, :])
-            mul([(slab, width)], first=True)
-        coarse_now = red5(r)
+            scal2(it)
+            red4(r)
+        if not last:
+            next_image(STEPS[1])
+            mul_own(STEPS[1])
+        curved, energy_now, crossed = scal_sum(it) if last else scal3(it)
+        raw_coarse = direct3() if last else red5(r)
         if it == 0:
+            coarse_z = known + raw_coarse
+            coarse_image = coarse_z
             d[...] = z[slab:, :]
             curvature = curved
-            coarse_image = coarse_now
         else:
+            images = raw_coarse if it == 1 else raw_coarse + beta * images
+            coarse_z = known - step * images
             beta = energy_now / energy
             d[...] = z[slab:, :] + beta * d[...]
             curvature = curved + beta * (2.0 * crossed + beta * curvature)
-            coarse_image = coarse_now + beta * coarse_image
+            coarse_image = coarse_z + beta * coarse_image
         energy = energy_now
         step = energy / curvature
         lam[...] += step * d[...]
         shift = dot(ginv, coarse_image)
         amp = amp - step * shift
         if not last:
-            bases(right_operand(shift), step, beta, it)
-            z[slab:, :] = zbase[slab:, :] - step * img[it + 1, slab:, :]
-            red1(r + 1, coarse(narrow(z[slab:, :])))
+            op = right_operand(shift)
+            bases(op, step, beta, it)
+            next_image(STEPS[2])
+            local = coarse(narrow(img[it + 1, slab:, :]))
+            if it + 1 < ITERS - 1:
+                red1(r + 1, local)
+            else:
+                direct1(local)
+            own_z(op, step, beta, it)
+            own_scalars(it + 1, beta)
+            mul_own(STEPS[2])
+            known = coarse_z + step * dot(cfc[...], shift)
+            if it + 1 < ITERS - 1:
+                red2(r + 1)
 
     amp_out[...] = amp
     out_lam = pltpu.make_async_copy(lam, lam_hbm, s["load_sem"].at[0])
@@ -565,7 +680,10 @@
         wait_for(pb, ny - 1, s["rs"].at[r, 1])
         wait_for(ga, ny - 1, s["rs"].at[r, 2])
         wait_for(gb, nx - 1, s["rs"].at[r, 3])
-    for it in range(ITERS):
+    wait_for(s["scal_a"], n - 1, s["ss"].at[ITERS - 1, 0])
+    wait_for(s["dp"], n - 1, s["ds"].at[0])
+    wait_for(s["dt"], n - 1, s["ds"].at[1])
+    for it in range(ITERS - 1):
         wait_for(scal_x.at[it], nx - 1, s["ss"].at[it, 0])
         wait_for(scal_y.at[it], ny - 1, s["ss"].at[it, 1])
     out_lam.wait()
@@ -586,13 +704,14 @@
         width = schur_blocks.shape[1]
         span = slab - slab // 4
         vmem, dma = pltpu.VMEM, pltpu.SemaphoreType.DMA
-        scratch = {"stage%d" % i: vmem((CHUNK, width), F32) for i in range(SLOTS)}
+        scratch = {"stage%d" % i: vmem((GROUP, width), F32) for i in range(SLOTS)}
         scratch |= {name: vmem((width, width), BF16) for name in ("s_hi", "s_lo")}
         scratch |= {name: vmem((width, 2 * nc), BF16) for name in ("vec", "basis_hl", "sc_hl")}
-        scratch |= {name: vmem((width, r), F32) for name in ("basis_w", "sc", "p", "z", "base", "zbase", "si")}
+        scratch |= {name: vmem((width, r), F32) for name in ("sc", "p", "z", "base", "zbase", "si")}
         scratch |= {name: vmem((slab, r), F32) for name in ("right", "basis_own", "lam", "d", "fc", "image")}
-        scratch |= {name: vmem((nc, r), F32) for name in ("load", "amp", "sweep")}
+        scratch |= {name: vmem((nc, r), F32) for name in ("load", "amp", "sweep", "cfc")}
         scratch |= {name: vmem((nc, slab), BF16) for name in ("fct_hi", "fct_lo")}
+        scratch |= {name: vmem((nc, width), BF16) for name in ("bt_hi", "bt_lo")}
         scratch |= {
             "twice": vmem((2 * width, r), F32),
             "img": vmem((IMAGES, width, r), F32),
@@ -603,6 +722,7 @@
             "m": vmem((2 * nc, r), F32),
             "scal_in": vmem((ITERS, 4, r), F32),
             "scal_mid": vmem((ITERS, 4, r), F32),
+            "scal_a": vmem((nx * ny, 4, r), F32),
             "scal_x": vmem((ITERS, nx, 4, r), F32),
             "scal_y": vmem((ITERS, ny, 4, r), F32),
         }
@@ -617,8 +737,11 @@
                 "ga%d" % k: vmem((ny, p, r), F32),
                 "gb%d" % k: vmem((nx, ny, p, r), F32),
             }
+        scratch |= {name: vmem((nx * ny, nc // (nx * ny), r), F32) for name in ("dp", "df", "dt")}
         scratch |= {name: dma((EXCHANGES, 3)) for name in ("hs_l", "hs_r", "hr_l", "hr_r")}
         scratch |= {
+            "ds": dma((2,)),
+            "dr": dma((2,)),
             "stage_sem": dma((SLOTS,)),
             "load_sem": dma((3,)),
             "rs": dma((REDUCES, 4)),

time: 115 us -> 99.8 us (0.87)
  Pallas kernels: 110 us -> 94.9 us
    pallas_call x1, Pallas kernels: 110 us -> 94.9 us  [local(): pl.pallas_call(functools.partial(entry, nx, ny, names), out_shape=(jax.Sh...]
where the time goes in v2:
time: 99.8 us; the launch traced here: 99.5 us
  Pallas kernels  94.9 us (95%)
  local copies, waits for them, and re-layouts  3.34 us (3%)
  between operations  1.29 us (1%)
    pallas_call x1, Pallas kernels, local(): pl.pallas_call(functools.partial(entry, nx, ny, names), out_shape=(jax.Sh...  94.9 us
    unnamed x2, local copies, waits for them, and re-layouts  3.34 us

profile of v2, /device:TPU:0, one launch (start us, length us, event | category | flops | bytes accessed | tf_op | source)
XLA Modules:
  0.0 99.5 jit_solution(5060949048860241138)
XLA Ops:
  1.3 94.9 %projected_cg.1 = (f32[1024,128]{1,0:T(8,128)}, f32[128,128]{1,0:T(8,128)}) custom-call(s32[1]{0:T(128)S(6)} %copy.9.refs_0_, f32[2048,2048]{1,0:T(8,128)} %bitcast.1, f32[1024,128]{1,0:T(8,128)} %refs_2_.1, f32[1024,128]{1,0:T(8,128)} %refs_3_.1, f32[128,128]{1,0:T(8,128)} %refs_4_.1), custom_call_target="tpu_custom_call" | custom-call | tf_op jit(solution)/shard_map/projected_cg/pallas_call | solution.py:754
  96.2 1.9 %copy.10 = f32[1024,128]{1,0:T(8,128)} copy(f32[1024,128]{1,0:T(8,128)} %get-tuple-element.4) | data formatting | bytes 1048576
  98.0 1.5 %copy.11 = f32[128,128]{1,0:T(8,128)} copy(f32[128,128]{1,0:T(8,128)} %get-tuple-element.5) | data formatting | bytes 131072

commit v3 on v2

--- a/solution.py
+++ b/solution.py
@@ -16,7 +16,7 @@
 CHUNK = 128
 SLOTS = 2
 GROUP = 512
-BLOCK = 512
+BLOCK = 1024
 PIVOTS = 4
 EXCHANGES = 3 + 2 * (ITERS - 1)
 PARTS = ITERS
@@ -431,9 +431,7 @@
             send_parts(1, 0, c, head)
             sc[q(c), :] = head
     for c in STEPS[2]:
-        head = folded(c * low, low)
-        send_parts(1, 0, c, head)
-        sc[q(c), :] = head
+        sc[q(c), :] = folded(c * low, low)
     sc[slab:, :] = folded(slab, slab)
     sc_hl[...] = narrow(sc[...])
     both = jnp.dot(s["bt_hi"][...], sc_hl[...], preferred_element_type=F32)
@@ -474,6 +472,8 @@
 
     half_way = lax.fori_loop(0, nc // PIVOTS // 2, pivot, sweep[...])
     red2(1)
+    for c in STEPS[2]:
+        send_parts(1, 0, c, sc[q(c), :])
     ginv = -lax.fori_loop(nc // PIVOTS // 2, nc // PIVOTS, pivot, half_way)
     load_in(2).wait()
     y0 = dot(ginv, load[...])
@@ -576,9 +576,6 @@
                 own_scalars(0, None)
                 bases(op, None, None, 0)
 
-        if last:
-            direct2()
-
         def next_p(c):
             p_c = base[q(c), :] + scale * folded(c * low, low)
             p_ref[q(c), :] = p_c
@@ -594,6 +591,7 @@
         scal_in[it, 0:1] = jnp.sum(z[...] * p_ref[...], axis=0, keepdims=True)
         if last:
             scal_all(it)
+            direct2()
         else:
             scal1(it)
         if not last:
@@ -623,6 +621,13 @@
         if not last:
             next_image(STEPS[1])
             mul_own(STEPS[1])
+            next_image(STEPS[2])
+            local = coarse(narrow(img[it + 1, slab:, :]))
+            if it + 1 < ITERS - 1:
+                red1(r + 1, local)
+            else:
+                direct1(local)
+            mul_own(STEPS[2])
         curved, energy_now, crossed = scal_sum(it) if last else scal3(it)
         raw_coarse = direct3() if last else red5(r)
         if it == 0:
@@ -644,19 +649,12 @@
         amp = amp - step * shift
         if not last:
             op = right_operand(shift)
-            bases(op, step, beta, it)
-            next_image(STEPS[2])
-            local = coarse(narrow(img[it + 1, slab:, :]))
-            if it + 1 < ITERS - 1:
-                red1(r + 1, local)
-            else:
-                direct1(local)
             own_z(op, step, beta, it)
             own_scalars(it + 1, beta)
-            mul_own(STEPS[2])
-            known = coarse_z + step * dot(cfc[...], shift)
             if it + 1 < ITERS - 1:
                 red2(r + 1)
+            bases(op, step, beta, it)
+            known = coarse_z + step * dot(cfc[...], shift)
 
     amp_out[...] = amp
     out_lam = pltpu.make_async_copy(lam, lam_hbm, s["load_sem"].at[0])
@@ -688,6 +686,24 @@
         wait_for(scal_y.at[it], ny - 1, s["ss"].at[it, 1])
     out_lam.wait()
     out_amp.wait()
+
+
+def finish(lam_in, amp_in, lam_out, amp_out, lam, amp, sems):
+    arrive = [
+        pltpu.make_async_copy(lam_in, lam, sems.at[0]),
+        pltpu.make_async_copy(amp_in, amp, sems.at[1]),
+    ]
+    leave = [
+        pltpu.make_async_copy(lam, lam_out, sems.at[2]),
+        pltpu.make_async_copy(amp, amp_out, sems.at[3]),
+    ]
+    for copy in arrive:
+        copy.start()
+    for there, back in zip(arrive, leave):
+        there.wait()
+        back.start()
+    for copy in leave:
+        copy.wait()
 
 
 def entry(nx, ny, names, *refs):
@@ -751,7 +767,7 @@
         }
         names = tuple(scratch)
         hbm = pl.BlockSpec(memory_space=pl.ANY)
-        return pl.pallas_call(
+        found = pl.pallas_call(
             functools.partial(entry, nx, ny, names),
             out_shape=(
                 jax.ShapeDtypeStruct((slab, r), F32),
@@ -765,6 +781,18 @@
             ),
             name="projected_cg",
         )(offsets, schur_blocks[0], right_side, coarse_basis, coarse_load)
+        return pl.pallas_call(
+            finish,
+            out_shape=(
+                jax.ShapeDtypeStruct((slab, r), F32),
+                jax.ShapeDtypeStruct((nc, r), F32),
+            ),
+            in_specs=[hbm, hbm],
+            out_specs=(hbm, hbm),
+            scratch_shapes=[vmem((slab, r), F32), vmem((nc, r), F32), dma((4,))],
+            compiler_params=pltpu.CompilerParams(vmem_limit_bytes=2 * 1024 * 1024),
+            name="finish",
+        )(*found)
 
     in_specs = (
         P(("gx", "gy"), None, None),

time: 99.8 us -> 99.1 us (level)
  local copies, waits for them, and re-layouts: 3.34 us -> 1.87 us
    unnamed x2 -> x4, local copies, waits for them, and re-layouts: 3.34 us -> 1.87 us
where the time goes in v3:
time: 99.1 us; the launch traced here: 98.9 us
  Pallas kernels  95.5 us (96%)
  local copies, waits for them, and re-layouts  1.87 us (2%)
  between operations  1.49 us (2%)
    pallas_call x1, Pallas kernels, local(): pl.pallas_call(functools.partial(entry, nx, ny, names), out_shape=(jax.Sh...  94.6 us

profile of v3, /device:TPU:0, one launch (start us, length us, event | category | flops | bytes accessed | tf_op | source)
XLA Modules:
  0.0 98.9 jit_solution(4157992611732957212)
XLA Ops:
  1.3 94.6 %projected_cg.1 = (f32[1024,128]{1,0:T(8,128)}, f32[128,128]{1,0:T(8,128)}) custom-call(s32[1]{0:T(128)S(6)} %copy.7.refs_0_, f32[2048,2048]{1,0:T(8,128)} %bitcast.1, f32[1024,128]{1,0:T(8,128)} %refs_2_.1, f32[1024,128]{1,0:T(8,128)} %refs_3_.1, f32[128,128]{1,0:T(8,128)} %refs_4_.1), custom_call_target="tpu_custom_call" | custom-call | tf_op jit(solution)/shard_map/projected_cg/pallas_call | solution.py:770
  95.8 0.0 copy-start
  95.9 1.0 %copy-done = f32[1024,128]{1,0:T(8,128)S(1)} copy-done((f32[1024,128]{1,0:T(8,128)S(1)}, f32[1024,128]{1,0:T(8,128)}, u32[]{:S(2)}) %copy-start) | copy-done | bytes 524312
  96.9 0.0 copy-start.1
  96.9 0.8 copy-done.1
  97.7 1.0 finish.1
Async XLA Ops:
  95.8 1.0 %copy-start = (f32[1024,128]{1,0:T(8,128)S(1)}, f32[1024,128]{1,0:T(8,128)}, u32[]{:S(2)}) copy-start(f32[1024,128]{1,0:T(8,128)} %get-tuple-element.4.lam_in) | copy-start | bytes 1572868
  96.9 0.8 copy-start.1
